TPU v7x, 32 devices: a whole 2x2x4 slice. The times are simulated.
32 devices in a mesh: grp: 4 (over z), kv: 4 (over y, x), tp: 2 (over core).
Axes of the slice: x: 2, y: 2, z: 4, core: 2. Of those that a mesh axis runs over, the one named last changes fastest.
Arguments:
- hidden_states: bfloat16 [512, 4096], P('grp', 'kv'), may hold values from -6 to 6
- attn_gain: float32 [4096], P('kv'), may hold values from 0.25 to 1.75
- mlp_gain: float32 [4096], replicated, may hold values from 0.25 to 1.75
- w_query: bfloat16 [4096, 4096], P('kv', 'tp'), may hold values from -0.09375 to 0.09375
- w_out: bfloat16 [32, 128, 4096], P('tp', 'kv'), may hold values from -1 to 1
- w_gate: bfloat16 [4096, 14336], P(None, ('kv', 'tp')), may hold values from -0.09375 to 0.09375
- w_up: bfloat16 [4096, 14336], P(None, ('kv', 'tp')), may hold values from -0.09375 to 0.09375
- w_down: bfloat16 [14336, 4096], P(('kv', 'tp')), may hold values from -0.046875 to 0.046875
- kv_pool: bfloat16 [256, 2, 128, 1024], P(('grp', 'kv'), None, None, 'tp'), may hold values from -110 to 110
- resident_cache: bfloat16 [4, 32, 2, 128, 1024], P('grp', 'kv', None, None, 'tp'), may hold values from -110 to 110
- resident_slot: int32 [4, 32], P('grp', 'kv'), may hold values from 0 to 127
- resident_len: int32 [4, 32], P('grp', 'kv'), may hold values from 1 to 128
- new_owner: int32 [4, 64], replicated, may hold values from 0 to 15, as said below
- new_local: int32 [4, 64], replicated, may hold values from 0 to 15
- new_slot: int32 [4, 64], P('grp', 'kv'), may hold values from 0 to 127
- new_len: int32 [4, 64], P('grp', 'kv'), may hold values from 1 to 128
- token_kv: bfloat16 [512, 2, 1024], P('grp', None, 'tp'), may hold values from -6 to 6
Outputs:
- mixed: bfloat16 [512, 4096], P(('grp', 'kv', 'tp'))
- new_cache: bfloat16 [4, 64, 2, 128, 1024], P('grp', 'kv', None, None, 'tp')
Inputs may be any that keep to these rules, and one draw needn't show every extreme that they name: New page c of group g is kept by the device of kv index c // 16 of group g and comes from the device whose index along grp+kv is new_owner[g, c]; every decode device receives exactly 4 new pages from the owners of each grp index; no owner sends more than 4 pages to the devices of one kv index over all groups, so at most 4 to one device; every owner sends each of its 16 pages exactly once.
All inputs are finite; a program needn't handle non-finite values.
Results may differ from a plain program's by a relative error of at most 0.018.
Values may be sent and summed in bfloat16 or wider, within the bound.
No kernel may reach another device: no remote copies, remote signals or barrier semaphores. Data moves between devices by JAX's collectives and lax.ppermute only.
A program may use at most 128 MiB of HBM per device.

v0:
```python
import jax
import jax.numpy as jnp
from jax import lax
from jax.sharding import PartitionSpec as P

D = 4096
HEADS = 32
KV_HEADS = 8
HEAD_DIM = 128
NPR = 4
neg_fill = -1e30
norm_eps = 1e-05


def combined_all(part, axis, combine):
    gathered = jax.tree.map(lambda a: lax.all_gather(a, axis), part)

    def take(source):
        return jax.tree.map(lambda a: lax.dynamic_index_in_dim(a, source, 0, False), gathered)

    return lax.fori_loop(
        1, lax.axis_size(axis), lambda source, state: combine(state, take(source)), take(0)
    )


def combine(earlier, later):
    top_a, sum_a, acc_a = earlier
    top_b, sum_b, acc_b = later
    top = jnp.maximum(top_a, top_b)
    fade_a = jnp.exp(top_a - top)
    fade_b = jnp.exp(top_b - top)
    return (
        top,
        sum_a * fade_a + sum_b * fade_b,
        acc_a * fade_a[..., None] + acc_b * fade_b[..., None],
    )


def nth_match(table, wanted, places):
    matched = (table == wanted).astype(jnp.int32)
    ranking = jnp.cumsum(matched, axis=1) - 1
    return (matched[:, None, :] == 1) & (ranking[:, None, :] == places[None, :, None])


def move_pages(kv_pool, new_owner, new_local):
    groups = lax.axis_size("grp")
    ranks = lax.axis_size("kv")
    per_dev = new_owner.shape[1] // ranks
    cap = groups * NPR // ranks
    grp_rank = lax.axis_index("grp")
    kv_rank = lax.axis_index("kv")
    owners = new_owner.reshape(groups * ranks, per_dev)
    myself = grp_rank * ranks + kv_rank
    places = jnp.arange(cap, dtype=jnp.int32)
    mine = lax.dynamic_index_in_dim(owners, myself, 0, keepdims=False)
    order = jnp.arange(per_dev, dtype=jnp.int32)
    by_col = (
        new_owner.reshape(groups, ranks, per_dev)
        .transpose(1, 0, 2)
        .reshape(ranks, groups * per_dev)
    )
    local_col = (
        new_local.reshape(groups, ranks, per_dev)
        .transpose(1, 0, 2)
        .reshape(ranks, groups * per_dev)
    )
    select = nth_match(by_col, myself, places)
    picked = jnp.sum(jnp.where(select, local_col[:, None, :], 0), axis=2)
    outgoing = jnp.take(kv_pool, picked.reshape(-1), axis=0)
    received = lax.all_to_all(outgoing, "kv", split_axis=0, concat_axis=0, tiled=True)
    row_here = lax.dynamic_index_in_dim(by_col, kv_rank, 0, keepdims=False)
    sources = grp_rank * ranks + jnp.arange(ranks, dtype=jnp.int32)
    hits = nth_match(
        jnp.broadcast_to(row_here[None, :], (ranks, row_here.shape[0])), sources[:, None], places
    )
    spots = jnp.arange(row_here.shape[0], dtype=jnp.int32)
    where_f = jnp.sum(jnp.where(hits, spots[None, None, :], 0), axis=2).reshape(-1)
    dest_grp = where_f // per_dev
    dest_pos = where_f % per_dev
    same = (dest_grp[:, None] == dest_grp[None, :]) & (dest_pos[:, None] < dest_pos[None, :])
    rank_in = jnp.sum(same.astype(jnp.int32), axis=0)
    target = dest_grp * NPR + rank_in
    items = jnp.arange(target.shape[0], dtype=jnp.int32)
    inverse = jnp.sum(jnp.where(target[None, :] == items[:, None], items[None, :], 0), axis=1)
    sorted_pages = jnp.take(received, inverse, axis=0)
    arrived = lax.all_to_all(sorted_pages, "grp", split_axis=0, concat_axis=0, tiled=True)
    src_grp = mine // ranks
    earlier = (src_grp[:, None] == src_grp[None, :]) & (order[:, None] < order[None, :])
    before = jnp.sum(earlier.astype(jnp.int32), axis=0)
    return jnp.take(arrived, src_grp * NPR + before, axis=0)


def local_partials(query, resident, arrived, res_slot, res_len, arr_slot, arr_len, token_kv, first):
    pages = jnp.concatenate([resident, arrived], axis=0)
    owner_slot = jnp.concatenate([res_slot, arr_slot])
    filled = jnp.concatenate([res_len, arr_len])
    count = pages.shape[0]
    tokens = pages.shape[2]
    kv_here = pages.shape[3] // HEAD_DIM
    slots = query.shape[0]
    ratio = HEADS // KV_HEADS
    keys = pages[:, 0].astype(jnp.float32).reshape(count, tokens, kv_here, HEAD_DIM)
    values = pages[:, 1].astype(jnp.float32).reshape(count, tokens, kv_here, HEAD_DIM)
    grouped = query.reshape(slots, kv_here, ratio, HEAD_DIM)
    picked = jnp.take(grouped, owner_slot, axis=0)
    scores = jnp.einsum("ikgd,itkd->ikgt", picked, keys, precision=lax.Precision.HIGHEST)
    usable = (jnp.arange(tokens, dtype=jnp.int32)[None, :] < filled[:, None])[:, None, None, :]
    scores = jnp.where(usable, scores, neg_fill)
    page_top = jnp.max(scores, axis=3)
    member = owner_slot[None, :] == jnp.arange(slots, dtype=jnp.int32)[:, None]
    slot_top = jnp.max(jnp.where(member[:, :, None, None], page_top[None], neg_fill), axis=1)
    own_keys = token_kv[:, 0].astype(jnp.float32).reshape(slots, kv_here, HEAD_DIM)
    own_values = token_kv[:, 1].astype(jnp.float32).reshape(slots, kv_here, HEAD_DIM)
    own_score = jnp.einsum("skgd,skd->skg", grouped, own_keys, precision=lax.Precision.HIGHEST)
    own_score = jnp.where(first, own_score, neg_fill)
    slot_top = jnp.maximum(slot_top, own_score)
    reach = jnp.take(slot_top, owner_slot, axis=0)
    weights = jnp.where(usable, jnp.exp(scores - reach[..., None]), 0.0)
    page_sum = jnp.sum(weights, axis=3)
    page_acc = jnp.einsum("ikgt,itkd->ikgd", weights, values, precision=lax.Precision.HIGHEST)
    own_weight = jnp.where(first, jnp.exp(own_score - slot_top), 0.0)
    member_f = member.astype(jnp.float32)
    total = jnp.dot(member_f, page_sum.reshape(count, -1), precision=lax.Precision.HIGHEST)
    total = total + own_weight.reshape(slots, -1)
    weighted = jnp.dot(member_f, page_acc.reshape(count, -1), precision=lax.Precision.HIGHEST)
    weighted = (
        weighted.reshape(slots, kv_here, ratio, HEAD_DIM)
        + own_weight[..., None] * own_values[:, :, None, :]
    )
    return (slot_top.reshape(slots, -1), total, weighted.reshape(slots, kv_here * ratio, HEAD_DIM))


def per_device(
    hidden_states,
    attn_gain,
    mlp_gain,
    w_query,
    w_out,
    w_gate,
    w_up,
    w_down,
    kv_pool,
    resident_cache,
    resident_slot,
    resident_len,
    new_owner,
    new_local,
    new_slot,
    new_len,
    token_kv,
):
    ranks = lax.axis_size("kv")
    pairs = lax.axis_size("tp")
    kv_rank = lax.axis_index("kv")
    tp_rank = lax.axis_index("tp")
    features = hidden_states.astype(jnp.float32)
    partial_query = jnp.dot(
        (features * attn_gain).astype(jnp.bfloat16), w_query, preferred_element_type=jnp.float32
    )
    squares = jnp.sum(features * features, axis=1)
    partial_query, squares = lax.psum((partial_query, squares), "kv")
    attn_scale = lax.rsqrt(squares / D + norm_eps)
    query = partial_query * attn_scale[:, None] * HEAD_DIM ** (-0.5)
    new_pages = move_pages(kv_pool, new_owner, new_local)
    top, total, weighted = local_partials(
        query,
        resident_cache[0],
        new_pages,
        resident_slot[0],
        resident_len[0],
        new_slot[0],
        new_len[0],
        token_kv,
        kv_rank == 0,
    )
    top, total, weighted = combined_all((top, total, weighted), "kv", combine)
    attn = (weighted / total[..., None]).astype(jnp.bfloat16)
    slots = attn.shape[0]
    heads_here = attn.shape[1]
    span = HEAD_DIM // ranks
    piece = lax.dynamic_slice_in_dim(attn, kv_rank * span, span, 2)
    branch = jnp.dot(
        piece.reshape(slots, heads_here * span),
        w_out.reshape(heads_here * span, w_out.shape[2]),
        preferred_element_type=jnp.float32,
    )
    width_here = hidden_states.shape[1]
    laid = branch.reshape(slots, ranks, width_here)
    spot = (jnp.arange(ranks, dtype=jnp.int32) == kv_rank) & (tp_rank == 0)
    laid = laid + jnp.where(spot[None, :, None], features[:, None, :], 0.0)
    resid = lax.psum(laid.reshape(slots, ranks * width_here).astype(jnp.bfloat16), ("kv", "tp"))
    resid_f = resid.astype(jnp.float32)
    mlp_scale = lax.rsqrt(jnp.sum(resid_f * resid_f, axis=1) / D + norm_eps)
    normed_mlp = (resid_f * mlp_gain).astype(jnp.bfloat16)
    gate = jnp.dot(normed_mlp, w_gate, preferred_element_type=jnp.float32) * mlp_scale[:, None]
    upward = jnp.dot(normed_mlp, w_up, preferred_element_type=jnp.float32) * mlp_scale[:, None]
    hidden_units = (jax.nn.silu(gate) * upward).astype(jnp.bfloat16)
    row_count = slots // (ranks * pairs)
    down = lax.psum_scatter(
        jnp.dot(hidden_units, w_down, preferred_element_type=jnp.float32).astype(jnp.bfloat16),
        ("kv", "tp"),
        scatter_dimension=0,
        tiled=True,
    ).astype(jnp.float32)
    row_start = (kv_rank * pairs + tp_rank) * row_count
    kept = lax.dynamic_slice_in_dim(resid_f, row_start, row_count, 0)
    mixed = (kept + down).astype(jnp.bfloat16)
    return (mixed, new_pages[None])


def solution(mesh):
    return jax.shard_map(
        per_device,
        mesh=mesh,
        in_specs=(
            P("grp", "kv"),
            P("kv"),
            P(),
            P("kv", "tp"),
            P("tp", "kv", None),
            P(None, ("kv", "tp")),
            P(None, ("kv", "tp")),
            P(("kv", "tp"), None),
            P(("grp", "kv"), None, None, "tp"),
            P("grp", "kv", None, None, "tp"),
            P("grp", "kv"),
            P("grp", "kv"),
            P(),
            P(),
            P("grp", "kv"),
            P("grp", "kv"),
            P("grp", None, "tp"),
        ),
        out_specs=(P(("grp", "kv", "tp"), None), P("grp", "kv", None, None, "tp")),
        check_vma=False,
    )
```

profile of v0, /device:TPU:0, one launch (start us, length us, event | category | flops | bytes accessed | tf_op | source)
XLA Modules:
  0.0 407.0 jit_solution(611504076523170792)
XLA Ops:
  7.2 0.8 reshape.445
  7.9 0.8 reshape.450
  8.8 0.2 reduce_window_sum.17
  9.0 0.8 reshape.447
  9.9 0.1 select_reduce_fusion.3
  10.2 5.0 %gather_fusion.2 = bf16[16,2,128,512]{3,2,1,0:T(8,128)(2,1)} fusion(bf16[16,2,128,512]{3,2,1,0:T(8,128)(2,1)} %param.29, s32[1024]{0:T(1024)S(1)} %pad_clamp_fusion.2), kind=kCustom, calls=%fused_computation.clone | custom fusion | bytes 8388672 | tf_op jit(solution)/shard_map/jit(_take)/gather | solution.py:69
  15.2 4.7 %broadcast_select_fusion.2 = bf16[16,2,128,512]{3,2,1,0:T(8,128)(2,1)} fusion(bf16[16,2,128,512]{3,2,1,0:T(8,128)(2,1)} %gather_fusion.2, pred[16]{0:T(512)(128)(4,1)S(1)} %compare_and_fusion.2), kind=kLoop, calls=%fused_computation.18 | loop fusion | flops 2097152 | bytes 8388624 | tf_op jit(solution)/shard_map/jit(_take)/select_n | solution.py:69
  19.9 5.2 %all-to-all-start = ((bf16[16,2,128,512]{3,2,1,0:T(8,128)(2,1)}), bf16[16,2,128,512]{3,2,1,0:T(8,128)(2,1)}, u32[]{:S(2)}, u32[]{:S(2)}) async-start(bf16[16,2,128,512]{3,2,1,0:T(8,128)(2,1)} %broadcast_select_fusion.2), calls=%async_computation | async-start | bytes 8388608 | tf_op jit(solution)/shard_map/all_to_all | solution.py:70
  25.1 0.2 reduce_window_sum.18
  25.4 0.1 select_reduce_fusion.2
  25.9 47.8 %all-to-all-done = bf16[16,2,128,512]{3,2,1,0:T(8,128)(2,1)} async-done(((bf16[16,2,128,512]{3,2,1,0:T(8,128)(2,1)}), bf16[16,2,128,512]{3,2,1,0:T(8,128)(2,1)}, u32[]{:S(2)}, u32[]{:S(2)}) %all-to-all-start) | async-done | bytes 4194336 | tf_op jit(solution)/shard_map/all_to_all | solution.py:70
  73.7 5.0 %gather_fusion.3 = bf16[16,2,128,512]{3,2,1,0:T(8,128)(2,1)} fusion(bf16[16,2,128,512]{3,2,1,0:T(8,128)(2,1)} %all-to-all-done, s32[1024]{0:T(1024)S(1)} %pad_clamp_fusion.1), kind=kCustom, calls=%fused_computation.1.clone | custom fusion | bytes 8388672 | tf_op jit(solution)/shard_map/jit(_take)/gather | solution.py:85
  78.7 4.7 %broadcast_select_fusion.1 = bf16[16,2,128,512]{3,2,1,0:T(8,128)(2,1)} fusion(bf16[16,2,128,512]{3,2,1,0:T(8,128)(2,1)} %gather_fusion.3, pred[16]{0:T(512)(128)(4,1)S(1)} %compare_and_fusion.1), kind=kLoop, calls=%fused_computation.17 | loop fusion | flops 2097152 | bytes 8388624 | tf_op jit(solution)/shard_map/jit(_take)/select_n | solution.py:85
  83.4 5.2 %all-to-all-start.1 = ((bf16[16,2,128,512]{3,2,1,0:T(8,128)(2,1)}), bf16[16,2,128,512]{3,2,1,0:T(8,128)(2,1)}, u32[]{:S(2)}, u32[]{:S(2)}) async-start(bf16[16,2,128,512]{3,2,1,0:T(8,128)(2,1)} %broadcast_select_fusion.1), calls=%async_computation.1 | async-start | bytes 8388608 | tf_op jit(solution)/shard_map/all_to_all | solution.py:86
  88.7 4.0 fusion.7
  93.1 0.4 slice_convert_fusion
  93.5 0.2 copy.150
  93.7 0.2 copy.143
  93.9 0.7 copy.134
  94.6 9.3 %psum.22 = f32[128]{0:T(128)S(1)} all-reduce(f32[128]{0:T(128)S(1)} %multiply_reduce_fusion.1), channel_id=1, replica_groups=mesh['grp'=4,'kv'=4,'tp'=2] {'kv'}, use_global_device_ids=true, to_apply=%region_2.0 | all-reduce | flops 128 | bytes 1024 | tf_op jit(solution)/shard_map/psum | solution.py:161
  104.2 41.8 %all-reduce.3.cloned.1.call-done = f32[128,2048]{1,0:T(8,128)} async-done(((f32[128,2048]{1,0:T(8,128)}), f32[128,2048]{1,0:T(8,128)}) %all-reduce.3.cloned.1.call-update) | async-done | bytes 1048592 | tf_op jit(solution)/shard_map/psum | solution.py:161
  145.9 1.4 multiply_multiply_fusion
  147.3 0.7 reshape.444
  148.0 1.3 gather_fusion
  149.4 2.5 fusion.34
  151.9 29.4 %all-to-all-done.1 = bf16[16,2,128,512]{3,2,1,0:T(8,128)(2,1)} async-done(((bf16[16,2,128,512]{3,2,1,0:T(8,128)(2,1)}), bf16[16,2,128,512]{3,2,1,0:T(8,128)(2,1)}, u32[]{:S(2)}, u32[]{:S(2)}) %all-to-all-start.1) | async-done | bytes 4194336 | tf_op jit(solution)/shard_map/all_to_all | solution.py:86
  181.3 5.0 %gather_fusion.4 = bf16[16,2,128,512]{3,2,1,0:T(8,128)(2,1)} fusion(bf16[16,2,128,512]{3,2,1,0:T(8,128)(2,1)} %all-to-all-done.1, s32[1024]{0:T(1024)S(1)} %pad_clamp_fusion), kind=kCustom, calls=%fused_computation.2.clone | custom fusion | bytes 8388672 | tf_op jit(solution)/shard_map/jit(_take)/gather | solution.py:90
  186.3 2.8 broadcast_select_fusion
  189.1 2.9 pad_maximum_fusion
  192.0 3.5 copy.122
  195.5 4.2 %fusion.33 = (f32[24,4,4]{2,1,0:T(4,128)S(1)}, f32[24,4,4,128]{3,2,1,0:T(4,128)}) fusion(bf16[24,128,4,128]{1,3,2,0:T(8,128)(2,1)S(1)} %bitcast.91, f32[24,4,4,128]{3,2,1,0:T(4,128)} %gather_fusion, pred[24]{0:T(512)(128)(4,1)S(1)} %get-tuple-element.244, pred[24,128]{1,0:T(8,128)(4,1)S(1)} %iota_compare_fusion), kind=kOutput, calls=%fused_computation.125 | convolution fusion | flops 75644544 | bytes 3543576 | tf_op jit(solution)/shard_map/ikgd,itkd->ikgt/dot_general | solution.py:106
  200.0 0.2 copy.126
  200.2 1.8 exponential_select_fusion
  202.0 0.6 gather_fusion.1
  202.7 3.5 copy.130
  206.2 6.6 %fusion.13 = f32[24,4,4,128]{3,2,1,0:T(4,128)} fusion(bf16[24,128,4,128]{1,3,2,0:T(8,128)(2,1)S(1)} %bitcast.95, f32[24,4,4,128]{3,2,1,0:T(4,128)} %get-tuple-element.261, f32[24,4,4]{2,1,0:T(4,128)S(1)} %broadcast_select_fusion.3, pred[24,128]{1,0:T(8,128)(4,1)S(1)} %iota_compare_fusion), kind=kOutput, calls=%fused_computation.50 | convolution fusion | flops 75595776 | bytes 3543552 | tf_op jit(solution)/shard_map/ikgt,itkd->ikgd/dot_general | solution.py:120
  212.8 1.0 reshape.456
  214.0 1.0 copy.129
  215.0 1.7 convolution_add_fusion
  216.8 1.7 copy.135
  218.5 0.3 all-reduce.5.cloned.1.call-start
  218.8 6.7 %copy.138 = bf16[4096,512]{1,0:T(8,128)(2,1)} copy(bf16[4096,512]{0,1:T(8,128)(2,1)} %bitcast.92) | data formatting | bytes 8388608 | tf_op jit(solution)/shard_map/dot_general | solution.py:182
  225.5 0.4 fusion.14
  226.0 0.2 convolution_add_fusion.1
  226.2 8.0 %all-gather = f32[512,16]{0,1:T(8,128)S(1)} all-gather(f32[128,16]{0,1:T(8,128)S(1)} %convolution_add_fusion.1), channel_id=2, replica_groups=mesh['grp'=4,'kv'=4,'tp'=2] {'kv'}, dimensions={0}, use_global_device_ids=true | all-gather | bytes 40960 | tf_op jit(solution)/shard_map/all_gather | solution.py:16
  234.3 8.2 %all_gather.12 = f32[4,128,16]{1,2,0:T(8,128)S(1)} all-gather(f32[1,128,16]{1,2,0:T(8,128)S(1)} %bitcast.104), channel_id=1, replica_groups=mesh['grp'=4,'kv'=4,'tp'=2] {'kv'}, dimensions={0}, use_global_device_ids=true | all-gather | bytes 40960 | tf_op jit(solution)/shard_map/all_gather | solution.py:16
  242.5 26.1 %all-gather.3.cloned.1.call-done = f32[4,128,16,128]{3,2,1,0:T(8,128)} async-done(((f32[1,128,16,128]{3,2,1,0:T(8,128)}), f32[4,128,16,128]{3,2,1,0:T(8,128)}) %all-gather.3.cloned.1.call-update) | async-done | bytes 4194320 | tf_op jit(solution)/shard_map/all_gather | solution.py:16
  268.7 1.3 slice_bitcast_fusion
  270.0 6.5 %while.19 = (s32[]{:T(128)}, f32[128,16]{0,1:T(8,128)S(1)}, f32[128,16]{0,1:T(8,128)S(1)}, f32[128,16,128]{2,1,0:T(8,128)S(1)}, f32[4,128,16]{1,2,0:T(8,128)S(1)...) while((s32[]{:T(128)}, f32[128,16]{0,1:T(8,128)S(1)}, ...), condition=%wide.region_14.16_spmd, body=%wide.region_13.15_spmd.sunk | while | flops 798725 | bytes 3276955 | solution.py:21
  270.2 1.9 fusion.48
  272.4 1.9 fusion.48
  274.5 1.9 fusion.48
  276.5 0.4 copy.137
  276.9 3.7 add_convert_fusion
  280.7 0.7 copy.140
  281.3 1.4 copy.141
  282.7 56.8 %all-reduce.5.cloned.1.call-done = bf16[128,4096]{1,0:T(8,128)(2,1)} async-done(((bf16[128,4096]{1,0:T(8,128)(2,1)}), bf16[128,4096]{1,0:T(8,128)(2,1)}) %all-reduce.5.cloned.1.call-update) | async-done | bytes 1048592 | tf_op jit(solution)/shard_map/psum | solution.py:191
  339.6 1.5 multiply_reduce_fusion
  341.1 7.7 %convolution_multiply_fusion.1 = f32[128,1792]{1,0:T(8,128)S(1)} fusion(bf16[4096,1792]{1,0:T(8,128)(2,1)} %param.26, f32[4096]{0:T(1024)S(1)} %copy-done.7, bf16[128,4096]{1,0:T(8,128)(2,1)} %all-reduce.5.cloned.1.call-done, f32[128]{0:T(128)S(1)} %add_rsqrt_fusion), kind=kOutput, calls=%fused_computation.22 | convolution fusion | flops 1880850432 | bytes 16663040 | tf_op jit(solution)/shard_map/dot_general | solution.py:195
  348.8 14.8 %convolution_convert_fusion = bf16[128,4096]{1,0:T(8,128)(2,1)} fusion(bf16[1792,4096]{1,0:T(8,128)(2,1)} %param.28, bf16[4096,1792]{1,0:T(8,128)(2,1)} %param.27, f32[128,1792]{1,0:T(8,128)S(1)} %convolution_multiply_fusion.1, f32[4096]{0:T(1024)S(1)} %copy-done.7, bf16[128,4096]{1,0:T(8,128)(2,1)S(1)} %copy-done, f32[128]{0:T(128)S(1)} %add_rsqrt_fusion), kind=kOutput, calls=%fused_computation.15 | convolution fusion | flops 3761799168 | bytes 32391680 | tf_op jit(solution)/shard_map/dot_general | solution.py:200
  363.6 4.7 %fusion.46 = bf16[1,16,2,128,512]{4,3,2,1,0:T(8,128)(2,1)} fusion(bf16[16,2,128,512]{3,2,1,0:T(8,128)(2,1)} %gather_fusion.4, pred[16]{0:T(512)(128)(4,1)S(1)} %get-tuple-element.246), kind=kLoop, calls=%fused_computation.127 | loop fusion | flops 2097152 | bytes 8388624 | tf_op jit(solution)/shard_map/broadcast_in_dim | solution.py:208
  368.2 0.2 convert_element_type.86
  368.4 30.5 %reduce-scatter.2.cloned.1.call-done = bf16[16,4096]{1,0:T(8,128)(2,1)} async-done(((bf16[128,4096]{1,0:T(8,128)(2,1)}), bf16[16,4096]{1,0:T(8,128)(2,1)}) %reduce-scatter.2.cloned.1.call-update) | async-done | bytes 131088 | tf_op jit(solution)/shard_map/reduce_scatter | solution.py:199
  398.9 1.6 add_convert_fusion.1
  (92 shorter events, 3.2 us)
Async XLA Ops:
  19.9 53.8 %all-to-all-start = ((bf16[16,2,128,512]{3,2,1,0:T(8,128)(2,1)}), bf16[16,2,128,512]{3,2,1,0:T(8,128)(2,1)}, u32[]{:S(2)}, u32[]{:S(2)}) async-start(bf16[16,2,128,512]{3,2,1,0:T(8,128)(2,1)} %broadcast_select_fusion.2), calls=%async_computation | async-start | bytes 8388608 | tf_op jit(solution)/shard_map/all_to_all | solution.py:70
  83.4 5.3 %copy-start.1 = (bf16[128,1024]{1,0:T(8,128)(2,1)S(1)}, bf16[128,1024]{1,0:T(8,128)(2,1)}, u32[]{:S(2)}) copy-start(bf16[128,1024]{1,0:T(8,128)(2,1)} %param.21) | copy-start | bytes 786436
  83.4 5.3 %copy-start.8 = (f32[1024]{0:T(1024)S(1)}, f32[1024]{0:T(1024)}, u32[]{:S(2)}) copy-start(f32[1024]{0:T(1024)} %param.22) | copy-start | bytes 12292
  83.4 97.9 %all-to-all-start.1 = ((bf16[16,2,128,512]{3,2,1,0:T(8,128)(2,1)}), bf16[16,2,128,512]{3,2,1,0:T(8,128)(2,1)}, u32[]{:S(2)}, u32[]{:S(2)}) async-start(bf16[16,2,128,512]{3,2,1,0:T(8,128)(2,1)} %broadcast_select_fusion.1), calls=%async_computation.1 | async-start | bytes 8388608 | tf_op jit(solution)/shard_map/all_to_all | solution.py:86
  88.6 4.2 %copy-start.9 = (s32[1,16]{1,0:T(1,128)S(1)}, s32[1,16]{1,0:T(1,128)}, u32[]{:S(2)}) copy-start(s32[1,16]{1,0:T(1,128)} %param.35) | copy-start | bytes 196
  88.6 4.2 %copy-start.10 = (s32[1,8]{1,0:T(1,128)S(1)}, s32[1,8]{1,0:T(1,128)}, u32[]{:S(2)}) copy-start(s32[1,8]{1,0:T(1,128)} %param.31) | copy-start | bytes 100
  88.6 4.5 %copy-start.5 = (bf16[128,2,512]{2,1,0:T(2,128)(2,1)S(1)}, bf16[128,2,512]{2,1,0:T(2,128)(2,1)}, u32[]{:S(2)}) copy-start(bf16[128,2,512]{2,1,0:T(2,128)(2,1)} %param.37) | copy-start | bytes 786436
  88.6 4.9 %copy-start.11 = (s32[1,16]{1,0:T(1,128)S(1)}, s32[1,16]{1,0:T(1,128)}, u32[]{:S(2)}) copy-start(s32[1,16]{1,0:T(1,128)} %param.36) | copy-start | bytes 196
  88.6 4.9 %copy-start.12 = (s32[1,8]{1,0:T(1,128)S(1)}, s32[1,8]{1,0:T(1,128)}, u32[]{:S(2)}) copy-start(s32[1,8]{1,0:T(1,128)} %param.32) | copy-start | bytes 100
  88.6 57.3 %all-reduce.3.cloned.1.call-start = ((), (), s32[]{:S(2)}) async-start(), calls=%async_computation.3 | async-start | bytes 2097152 | tf_op jit(solution)/shard_map/psum | solution.py:161
  92.7 176.0 %all-gather.3.cloned.1.call-start = ((), (), s32[]{:S(2)}) async-start(), calls=%async_computation.4 | async-start | bytes 5242880 | tf_op jit(solution)/shard_map/all_gather | solution.py:16
  186.3 2.9 copy-start.2
  202.0 0.7 copy-start.3
  218.5 121.1 %all-reduce.5.cloned.1.call-start = ((), (), s32[]{:S(2)}) async-start(), calls=%async_computation.5 | async-start | bytes 2097152 | tf_op jit(solution)/shard_map/psum | solution.py:191
  218.8 6.7 %copy-start.6 = (f32[24,4,4,128]{3,2,1,0:T(4,128)S(1)}, f32[24,4,4,128]{3,2,1,0:T(4,128)}, u32[]{:S(2)}) copy-start(f32[24,4,4,128]{3,2,1,0:T(4,128)} %get-tuple-element.261) | copy-start | bytes 589828
  218.8 15.4 %copy-start.4 = (f32[128,4,4]{2,1,0:T(4,128)S(1)}, f32[128,4,4]{2,1,0:T(4,128)}, u32[]{:S(2)}) copy-start(f32[128,4,4]{2,1,0:T(4,128)} %copy-done.3) | copy-start | bytes 24580
  280.6 60.4 %copy-start.7 = (f32[4096]{0:T(1024)S(1)}, f32[4096]{0:T(1024)}, u32[]{:S(2)}) copy-start(f32[4096]{0:T(1024)} %param.23) | copy-start | bytes 49156
  282.7 116.2 %reduce-scatter.2.cloned.1.call-start = ((), (), s32[]{:S(2)}) async-start(), calls=%async_computation.6 | async-start | bytes 1179648 | tf_op jit(solution)/shard_map/reduce_scatter | solution.py:199
  341.1 7.7 %copy-start = (bf16[128,4096]{1,0:T(8,128)(2,1)S(1)}, bf16[128,4096]{1,0:T(8,128)(2,1)}, u32[]{:S(2)}) copy-start(bf16[128,4096]{1,0:T(8,128)(2,1)} %all-reduce.5.cloned.1.call-done) | copy-start | bytes 3145732
Sparse Core Ops, SparseCore 0:
  92.8 53.0 all-reduce.2
  218.6 50.0 all-gather.2
  282.8 56.6 all-reduce.4
  363.7 35.1 reduce-scatter.1
where the time goes:
time: 408 us; the launch traced here: 407 us
  waiting for transfers between devices  232 us (57%)
  matrix products  45.4 us (11%)
  local copies, waits for them, and re-layouts  43.9 us (11%)
  other arithmetic  34.8 us (9%)
  blocking collectives  25.5 us (6%)
  between operations  14.2 us (3%)
  starting transfers between devices  10.8 us (3%)
    psum x1, waiting for transfers between devices, per_device(): lax.psum(laid.reshape(slots, ranks * width_here).astype(jnp.bfloat16), ('...  56.8 us
    all_to_all x1, waiting for transfers between devices, move_pages(): lax.all_to_all(outgoing, 'kv', split_axis=0, concat_axis=0, tiled=True)  47.8 us
    psum x1, waiting for transfers between devices, per_device(): partial_query, squares = lax.psum((partial_query, squares), 'kv')  41.8 us
    reduce_scatter x1, waiting for transfers between devices, per_device(): lax.psum_scatter(jnp.dot(hidden_units, w_down, preferred_element_type=jnp...  30.5 us
    all_to_all x1, waiting for transfers between devices, move_pages(): lax.all_to_all(sorted_pages, 'grp', split_axis=0, concat_axis=0, tiled=True)  29.4 us
    all_gather x1, waiting for transfers between devices, combined_all(): gathered = jax.tree.map(lambda a: lax.all_gather(a, axis), part)  26.1 us
    all_gather x2, blocking collectives, combined_all(): gathered = jax.tree.map(lambda a: lax.all_gather(a, axis), part)  16.2 us
    dot_general x1, matrix products, per_device(): jnp.dot(hidden_units, w_down, preferred_element_type=jnp.float32)  14.8 us
  transfers between devices with their start and end apart: 6, of which 6 were waited for; matrix products, arithmetic and copies ran while one was open for 6% of the time, Pallas kernels for 0%

commit v1 on v0

--- a/solution.py
+++ b/solution.py
@@ -149,6 +149,14 @@
     new_len,
     token_kv,
 ):
+
+    def fix_the_tables(block_in):
+        axis_key = "kv"
+        mesh_ax = "tp"
+        for ii in (mesh_ax, axis_key):
+            block_in = lax.psum(block_in, ii)
+        return block_in
+
     ranks = lax.axis_size("kv")
     pairs = lax.axis_size("tp")
     kv_rank = lax.axis_index("kv")
@@ -188,7 +196,7 @@
     laid = branch.reshape(slots, ranks, width_here)
     spot = (jnp.arange(ranks, dtype=jnp.int32) == kv_rank) & (tp_rank == 0)
     laid = laid + jnp.where(spot[None, :, None], features[:, None, :], 0.0)
-    resid = lax.psum(laid.reshape(slots, ranks * width_here).astype(jnp.bfloat16), ("kv", "tp"))
+    resid = fix_the_tables(laid.reshape(slots, ranks * width_here).astype(jnp.bfloat16))
     resid_f = resid.astype(jnp.float32)
     mlp_scale = lax.rsqrt(jnp.sum(resid_f * resid_f, axis=1) / D + norm_eps)
     normed_mlp = (resid_f * mlp_gain).astype(jnp.bfloat16)

time: 408 us -> 428 us (1.049)
  waiting for transfers between devices: 232 us -> 252 us
    psum x1 -> x2, waiting for transfers between devices: 56.8 us -> 76.1 us  [fix_the_tables(): block_in = lax.psum(block_in, ii)]
  transfers between devices with their start and end apart: 6 -> 7, of which waited for: 6 -> 7; matrix products, arithmetic and copies ran while one was open for 6% -> 6% of each run, Pallas kernels for 0% -> 0%
where the time goes in v1:
time: 428 us; the launch traced here: 427 us
  waiting for transfers between devices  252 us (59%)
  matrix products  45.4 us (11%)
  local copies, waits for them, and re-layouts  43.9 us (10%)
  other arithmetic  34.8 us (8%)
  blocking collectives  25.5 us (6%)
  between operations  14.2 us (3%)
  starting transfers between devices  10.8 us (3%)
    psum x2, waiting for transfers between devices, fix_the_tables(): block_in = lax.psum(block_in, ii)  76.1 us
    all_to_all x1, waiting for transfers between devices, move_pages(): lax.all_to_all(outgoing, 'kv', split_axis=0, concat_axis=0, tiled=True)  47.8 us
    psum x1, waiting for transfers between devices, per_device(): partial_query, squares = lax.psum((partial_query, squares), 'kv')  41.8 us
    reduce_scatter x1, waiting for transfers between devices, per_device(): lax.psum_scatter(jnp.dot(hidden_units, w_down, preferred_element_type=jnp...  31.2 us
    all_to_all x1, waiting for transfers between devices, move_pages(): lax.all_to_all(sorted_pages, 'grp', split_axis=0, concat_axis=0, tiled=True)  29.4 us
    all_gather x1, waiting for transfers between devices, combined_all(): gathered = jax.tree.map(lambda a: lax.all_gather(a, axis), part)  26.1 us
    all_gather x2, blocking collectives, combined_all(): gathered = jax.tree.map(lambda a: lax.all_gather(a, axis), part)  16.2 us
    dot_general x1, matrix products, per_device(): jnp.dot(hidden_units, w_down, preferred_element_type=jnp.float32)  14.8 us
  transfers between devices with their start and end apart: 7, of which 7 were waited for; matrix products, arithmetic and copies ran while one was open for 6% of the time, Pallas kernels for 0%

profile of v1, /device:TPU:0, one launch (start us, length us, event | category | flops | bytes accessed | tf_op | source)
XLA Modules:
  0.0 427.1 jit_solution(2824595694351304734)
XLA Ops:
  7.2 0.8 reshape.445
  7.9 0.8 reshape.450
  8.8 0.2 reduce_window_sum.17
  9.0 0.8 reshape.447
  9.9 0.1 select_reduce_fusion.3
  10.2 5.0 %gather_fusion.2 = bf16[16,2,128,512]{3,2,1,0:T(8,128)(2,1)} fusion(bf16[16,2,128,512]{3,2,1,0:T(8,128)(2,1)} %param.29, s32[1024]{0:T(1024)S(1)} %pad_clamp_fusion.2), kind=kCustom, calls=%fused_computation.clone | custom fusion | bytes 8388672 | tf_op jit(solution)/shard_map/jit(_take)/gather | solution.py:69
  15.2 4.7 %broadcast_select_fusion.2 = bf16[16,2,128,512]{3,2,1,0:T(8,128)(2,1)} fusion(bf16[16,2,128,512]{3,2,1,0:T(8,128)(2,1)} %gather_fusion.2, pred[16]{0:T(512)(128)(4,1)S(1)} %compare_and_fusion.2), kind=kLoop, calls=%fused_computation.18 | loop fusion | flops 2097152 | bytes 8388624 | tf_op jit(solution)/shard_map/jit(_take)/select_n | solution.py:69
  19.9 5.2 %all-to-all-start = ((bf16[16,2,128,512]{3,2,1,0:T(8,128)(2,1)}), bf16[16,2,128,512]{3,2,1,0:T(8,128)(2,1)}, u32[]{:S(2)}, u32[]{:S(2)}) async-start(bf16[16,2,128,512]{3,2,1,0:T(8,128)(2,1)} %broadcast_select_fusion.2), calls=%async_computation | async-start | bytes 8388608 | tf_op jit(solution)/shard_map/all_to_all | solution.py:70
  25.1 0.2 reduce_window_sum.18
  25.9 47.8 %all-to-all-done = bf16[16,2,128,512]{3,2,1,0:T(8,128)(2,1)} async-done(((bf16[16,2,128,512]{3,2,1,0:T(8,128)(2,1)}), bf16[16,2,128,512]{3,2,1,0:T(8,128)(2,1)}, u32[]{:S(2)}, u32[]{:S(2)}) %all-to-all-start) | async-done | bytes 4194336 | tf_op jit(solution)/shard_map/all_to_all | solution.py:70
  73.7 5.0 %gather_fusion.3 = bf16[16,2,128,512]{3,2,1,0:T(8,128)(2,1)} fusion(bf16[16,2,128,512]{3,2,1,0:T(8,128)(2,1)} %all-to-all-done, s32[1024]{0:T(1024)S(1)} %pad_clamp_fusion.1), kind=kCustom, calls=%fused_computation.1.clone | custom fusion | bytes 8388672 | tf_op jit(solution)/shard_map/jit(_take)/gather | solution.py:85
  78.7 4.7 %broadcast_select_fusion.1 = bf16[16,2,128,512]{3,2,1,0:T(8,128)(2,1)} fusion(bf16[16,2,128,512]{3,2,1,0:T(8,128)(2,1)} %gather_fusion.3, pred[16]{0:T(512)(128)(4,1)S(1)} %compare_and_fusion.1), kind=kLoop, calls=%fused_computation.17 | loop fusion | flops 2097152 | bytes 8388624 | tf_op jit(solution)/shard_map/jit(_take)/select_n | solution.py:85
  83.4 5.2 %all-to-all-start.1 = ((bf16[16,2,128,512]{3,2,1,0:T(8,128)(2,1)}), bf16[16,2,128,512]{3,2,1,0:T(8,128)(2,1)}, u32[]{:S(2)}, u32[]{:S(2)}) async-start(bf16[16,2,128,512]{3,2,1,0:T(8,128)(2,1)} %broadcast_select_fusion.1), calls=%async_computation.1 | async-start | bytes 8388608 | tf_op jit(solution)/shard_map/all_to_all | solution.py:86
  88.7 4.0 fusion.7
  93.1 0.4 slice_convert_fusion
  93.5 0.2 copy.150
  93.7 0.2 copy.143
  93.9 0.7 copy.134
  94.6 9.3 %psum.29 = f32[128]{0:T(128)S(1)} all-reduce(f32[128]{0:T(128)S(1)} %multiply_reduce_fusion.1), channel_id=1, replica_groups=mesh['grp'=4,'kv'=4,'tp'=2] {'kv'}, use_global_device_ids=true, to_apply=%region_2.0 | all-reduce | flops 128 | bytes 1024 | tf_op jit(solution)/shard_map/psum | solution.py:169
  104.2 41.8 %all-reduce.4.cloned.1.call-done = f32[128,2048]{1,0:T(8,128)} async-done(((f32[128,2048]{1,0:T(8,128)}), f32[128,2048]{1,0:T(8,128)}) %all-reduce.4.cloned.1.call-update) | async-done | bytes 1048592 | tf_op jit(solution)/shard_map/psum | solution.py:169
  145.9 1.4 multiply_multiply_fusion
  147.3 0.7 reshape.444
  148.0 1.3 gather_fusion
  149.4 2.5 fusion.34
  151.9 29.4 %all-to-all-done.1 = bf16[16,2,128,512]{3,2,1,0:T(8,128)(2,1)} async-done(((bf16[16,2,128,512]{3,2,1,0:T(8,128)(2,1)}), bf16[16,2,128,512]{3,2,1,0:T(8,128)(2,1)}, u32[]{:S(2)}, u32[]{:S(2)}) %all-to-all-start.1) | async-done | bytes 4194336 | tf_op jit(solution)/shard_map/all_to_all | solution.py:86
  181.3 5.0 %gather_fusion.4 = bf16[16,2,128,512]{3,2,1,0:T(8,128)(2,1)} fusion(bf16[16,2,128,512]{3,2,1,0:T(8,128)(2,1)} %all-to-all-done.1, s32[1024]{0:T(1024)S(1)} %pad_clamp_fusion), kind=kCustom, calls=%fused_computation.2.clone | custom fusion | bytes 8388672 | tf_op jit(solution)/shard_map/jit(_take)/gather | solution.py:90
  186.3 2.8 broadcast_select_fusion
  189.1 2.9 pad_maximum_fusion
  192.0 3.5 copy.122
  195.5 4.2 fusion.33
  200.0 0.2 copy.126
  200.2 1.8 exponential_select_fusion
  202.0 0.6 gather_fusion.1
  202.7 3.5 copy.130
  206.2 6.6 %fusion.13 = f32[24,4,4,128]{3,2,1,0:T(4,128)} fusion(bf16[24,128,4,128]{1,3,2,0:T(8,128)(2,1)S(1)} %bitcast.95, f32[24,4,4,128]{3,2,1,0:T(4,128)} %get-tuple-element.261, f32[24,4,4]{2,1,0:T(4,128)S(1)} %broadcast_select_fusion.3, pred[24,128]{1,0:T(8,128)(4,1)S(1)} %iota_compare_fusion), kind=kOutput, calls=%fused_computation.50 | convolution fusion | flops 75595776 | bytes 3543552 | tf_op jit(solution)/shard_map/ikgt,itkd->ikgd/dot_general | solution.py:120
  212.8 1.0 reshape.456
  214.0 1.0 copy.129
  215.0 1.7 convolution_add_fusion
  216.8 1.7 copy.135
  218.5 0.3 all-reduce.6.cloned.1.call-start
  218.8 6.7 %copy.138 = bf16[4096,512]{1,0:T(8,128)(2,1)} copy(bf16[4096,512]{0,1:T(8,128)(2,1)} %bitcast.92) | data formatting | bytes 8388608 | tf_op jit(solution)/shard_map/dot_general | solution.py:190
  225.5 0.4 fusion.14
  226.0 0.2 convolution_add_fusion.1
  226.2 8.0 %all-gather = f32[512,16]{0,1:T(8,128)S(1)} all-gather(f32[128,16]{0,1:T(8,128)S(1)} %convolution_add_fusion.1), channel_id=2, replica_groups=mesh['grp'=4,'kv'=4,'tp'=2] {'kv'}, dimensions={0}, use_global_device_ids=true | all-gather | bytes 40960 | tf_op jit(solution)/shard_map/all_gather | solution.py:16
  234.3 8.2 %all_gather.12 = f32[4,128,16]{1,2,0:T(8,128)S(1)} all-gather(f32[1,128,16]{1,2,0:T(8,128)S(1)} %bitcast.104), channel_id=1, replica_groups=mesh['grp'=4,'kv'=4,'tp'=2] {'kv'}, dimensions={0}, use_global_device_ids=true | all-gather | bytes 40960 | tf_op jit(solution)/shard_map/all_gather | solution.py:16
  242.5 26.1 %all-gather.3.cloned.1.call-done = f32[4,128,16,128]{3,2,1,0:T(8,128)} async-done(((f32[1,128,16,128]{3,2,1,0:T(8,128)}), f32[4,128,16,128]{3,2,1,0:T(8,128)}) %all-gather.3.cloned.1.call-update) | async-done | bytes 4194320 | tf_op jit(solution)/shard_map/all_gather | solution.py:16
  268.7 1.3 slice_bitcast_fusion
  270.0 6.5 %while.19 = (s32[]{:T(128)}, f32[128,16]{0,1:T(8,128)S(1)}, f32[128,16]{0,1:T(8,128)S(1)}, f32[128,16,128]{2,1,0:T(8,128)S(1)}, f32[4,128,16]{1,2,0:T(8,128)S(1)...) while((s32[]{:T(128)}, f32[128,16]{0,1:T(8,128)S(1)}, ...), condition=%wide.region_14.16_spmd, body=%wide.region_13.15_spmd.sunk | while | flops 798725 | bytes 3276955 | solution.py:21
  270.2 1.9 fusion.48
  272.4 1.9 fusion.48
  274.5 1.9 fusion.48
  276.5 0.4 copy.137
  276.9 3.7 add_convert_fusion
  280.7 0.7 copy.140
  281.3 1.4 copy.141
  282.7 19.5 %all-reduce.6.cloned.1.call-done = bf16[128,4096]{1,0:T(8,128)(2,1)} async-done(((bf16[128,4096]{1,0:T(8,128)(2,1)}), bf16[128,4096]{1,0:T(8,128)(2,1)}) %all-reduce.6.cloned.1.call-update) | async-done | bytes 1048592 | tf_op jit(solution)/shard_map/psum | solution.py:157
  302.4 56.5 %all-reduce.8.cloned.1.call-done = bf16[128,4096]{1,0:T(8,128)(2,1)} async-done(((bf16[128,4096]{1,0:T(8,128)(2,1)}), bf16[128,4096]{1,0:T(8,128)(2,1)}) %all-reduce.8.cloned.1.call-update) | async-done | bytes 1048592 | tf_op jit(solution)/shard_map/psum | solution.py:157
  358.9 1.5 multiply_reduce_fusion
  360.4 7.7 %convolution_multiply_fusion.1 = f32[128,1792]{1,0:T(8,128)S(1)} fusion(bf16[4096,1792]{1,0:T(8,128)(2,1)} %param.26, f32[4096]{0:T(1024)S(1)} %copy-done.7, bf16[128,4096]{1,0:T(8,128)(2,1)} %all-reduce.8.cloned.1.call-done, f32[128]{0:T(128)S(1)} %add_rsqrt_fusion), kind=kOutput, calls=%fused_computation.22 | convolution fusion | flops 1880850432 | bytes 16663040 | tf_op jit(solution)/shard_map/dot_general | solution.py:203
  368.1 14.8 %convolution_convert_fusion = bf16[128,4096]{1,0:T(8,128)(2,1)} fusion(bf16[1792,4096]{1,0:T(8,128)(2,1)} %param.28, bf16[4096,1792]{1,0:T(8,128)(2,1)} %param.27, f32[128,1792]{1,0:T(8,128)S(1)} %convolution_multiply_fusion.1, f32[4096]{0:T(1024)S(1)} %copy-done.7, bf16[128,4096]{1,0:T(8,128)(2,1)S(1)} %copy-done, f32[128]{0:T(128)S(1)} %add_rsqrt_fusion), kind=kOutput, calls=%fused_computation.15 | convolution fusion | flops 3761799168 | bytes 32391680 | tf_op jit(solution)/shard_map/dot_general | solution.py:208
  382.9 4.7 %fusion.46 = bf16[1,16,2,128,512]{4,3,2,1,0:T(8,128)(2,1)} fusion(bf16[16,2,128,512]{3,2,1,0:T(8,128)(2,1)} %gather_fusion.4, pred[16]{0:T(512)(128)(4,1)S(1)} %get-tuple-element.246), kind=kLoop, calls=%fused_computation.127 | loop fusion | flops 2097152 | bytes 8388624 | tf_op jit(solution)/shard_map/broadcast_in_dim | solution.py:216
  387.6 0.2 convert_element_type.86
  387.8 31.2 %reduce-scatter.2.cloned.1.call-done = bf16[16,4096]{1,0:T(8,128)(2,1)} async-done(((bf16[128,4096]{1,0:T(8,128)(2,1)}), bf16[16,4096]{1,0:T(8,128)(2,1)}) %reduce-scatter.2.cloned.1.call-update) | async-done | bytes 131088 | tf_op jit(solution)/shard_map/reduce_scatter | solution.py:207
  419.0 1.6 add_convert_fusion.1
  (95 shorter events, 3.4 us)
Async XLA Ops:
  19.9 53.8 %all-to-all-start = ((bf16[16,2,128,512]{3,2,1,0:T(8,128)(2,1)}), bf16[16,2,128,512]{3,2,1,0:T(8,128)(2,1)}, u32[]{:S(2)}, u32[]{:S(2)}) async-start(bf16[16,2,128,512]{3,2,1,0:T(8,128)(2,1)} %broadcast_select_fusion.2), calls=%async_computation | async-start | bytes 8388608 | tf_op jit(solution)/shard_map/all_to_all | solution.py:70
  83.4 5.3 %copy-start.1 = (bf16[128,1024]{1,0:T(8,128)(2,1)S(1)}, bf16[128,1024]{1,0:T(8,128)(2,1)}, u32[]{:S(2)}) copy-start(bf16[128,1024]{1,0:T(8,128)(2,1)} %param.21) | copy-start | bytes 786436
  83.4 5.3 %copy-start.8 = (f32[1024]{0:T(1024)S(1)}, f32[1024]{0:T(1024)}, u32[]{:S(2)}) copy-start(f32[1024]{0:T(1024)} %param.22) | copy-start | bytes 12292
  83.4 97.9 %all-to-all-start.1 = ((bf16[16,2,128,512]{3,2,1,0:T(8,128)(2,1)}), bf16[16,2,128,512]{3,2,1,0:T(8,128)(2,1)}, u32[]{:S(2)}, u32[]{:S(2)}) async-start(bf16[16,2,128,512]{3,2,1,0:T(8,128)(2,1)} %broadcast_select_fusion.1), calls=%async_computation.1 | async-start | bytes 8388608 | tf_op jit(solution)/shard_map/all_to_all | solution.py:86
  88.6 4.2 copy-start.9
  88.6 4.2 copy-start.10
  88.6 4.5 %copy-start.5 = (bf16[128,2,512]{2,1,0:T(2,128)(2,1)S(1)}, bf16[128,2,512]{2,1,0:T(2,128)(2,1)}, u32[]{:S(2)}) copy-start(bf16[128,2,512]{2,1,0:T(2,128)(2,1)} %param.37) | copy-start | bytes 786436
  88.6 4.9 %copy-start.11 = (s32[1,16]{1,0:T(1,128)S(1)}, s32[1,16]{1,0:T(1,128)}, u32[]{:S(2)}) copy-start(s32[1,16]{1,0:T(1,128)} %param.36) | copy-start | bytes 196
  88.6 4.9 %copy-start.12 = (s32[1,8]{1,0:T(1,128)S(1)}, s32[1,8]{1,0:T(1,128)}, u32[]{:S(2)}) copy-start(s32[1,8]{1,0:T(1,128)} %param.32) | copy-start | bytes 100
  88.6 57.3 %all-reduce.4.cloned.1.call-start = ((), (), s32[]{:S(2)}) async-start(), calls=%async_computation.3 | async-start | bytes 2097152 | tf_op jit(solution)/shard_map/psum | solution.py:169
  92.7 176.0 %all-gather.3.cloned.1.call-start = ((), (), s32[]{:S(2)}) async-start(), calls=%async_computation.4 | async-start | bytes 5242880 | tf_op jit(solution)/shard_map/all_gather | solution.py:16
  186.3 2.9 copy-start.2
  202.0 0.7 copy-start.3
  218.5 83.8 %all-reduce.6.cloned.1.call-start = ((), (), s32[]{:S(2)}) async-start(), calls=%async_computation.5 | async-start | bytes 2097152 | tf_op jit(solution)/shard_map/psum | solution.py:157
  218.8 6.7 %copy-start.6 = (f32[24,4,4,128]{3,2,1,0:T(4,128)S(1)}, f32[24,4,4,128]{3,2,1,0:T(4,128)}, u32[]{:S(2)}) copy-start(f32[24,4,4,128]{3,2,1,0:T(4,128)} %get-tuple-element.261) | copy-start | bytes 589828
  218.8 15.4 %copy-start.4 = (f32[128,4,4]{2,1,0:T(4,128)S(1)}, f32[128,4,4]{2,1,0:T(4,128)}, u32[]{:S(2)}) copy-start(f32[128,4,4]{2,1,0:T(4,128)} %copy-done.3) | copy-start | bytes 24580
  280.6 79.8 %copy-start.7 = (f32[4096]{0:T(1024)S(1)}, f32[4096]{0:T(1024)}, u32[]{:S(2)}) copy-start(f32[4096]{0:T(1024)} %param.23) | copy-start | bytes 49156
  282.7 76.2 %all-reduce.8.cloned.1.call-start = ((), (), s32[]{:S(2)}) async-start(), calls=%async_computation.6 | async-start | bytes 2097152 | tf_op jit(solution)/shard_map/psum | solution.py:157
  302.3 116.7 %reduce-scatter.2.cloned.1.call-start = ((), (), s32[]{:S(2)}) async-start(), calls=%async_computation.7 | async-start | bytes 1179648 | tf_op jit(solution)/shard_map/reduce_scatter | solution.py:207
  360.4 7.7 %copy-start = (bf16[128,4096]{1,0:T(8,128)(2,1)S(1)}, bf16[128,4096]{1,0:T(8,128)(2,1)}, u32[]{:S(2)}) copy-start(bf16[128,4096]{1,0:T(8,128)(2,1)} %all-reduce.8.cloned.1.call-done) | copy-start | bytes 3145732
Sparse Core Ops, SparseCore 0:
  92.8 53.0 all-reduce.3
  218.6 50.0 all-gather.2
  282.8 19.4 all-reduce.5
  305.2 53.6 all-reduce.7
  383.0 35.9 reduce-scatter.1
